TPU v7x, 256 devices: a whole 4x4x8 slice. The times are simulated.
256 devices in a mesh: seq: 2 (over core), batch: 128 (over z, y, x).
Axes of the slice: x: 4, y: 4, z: 8, core: 2. Of those that a mesh axis runs over, the one named last changes fastest.
Arguments:
- queries: bfloat16 [128, 1024, 1024], P('batch', 'seq'), may hold values from -6 to 6
- keys: bfloat16 [128, 1024, 1024], P('batch', 'seq'), may hold values from -6 to 6
- values: bfloat16 [128, 1024, 2048], P('batch', 'seq'), may hold values from -6 to 6
- gate_rate: bfloat16 [128, 1024, 1024], P('batch', 'seq'), may hold values from 0.5 to 2
- segment_ids: int32 [128, 1024], P('batch', 'seq'), may hold values from 0 to 2, never falling along the last dimension, each value on 1 to 512 neighbouring positions
- decay_exps: int32 [4], replicated, may hold values from 0 to 13
- out_weight: bfloat16 [2048, 2048], P('batch'), may hold values from -0.125 to 0.125
Outputs:
- projected: bfloat16 [128, 1024, 2048], P('batch', 'seq')
Inputs may be any that keep to these rules, and one draw needn't show every extreme that they name: `segment_ids`: within each stream the ids never fall and start at 0; each of the 3 ids covers 1 to 512 consecutive tokens, one of them exactly 512.
All inputs are finite; a program needn't handle non-finite values.
Results may differ from a plain program's by a relative error of at most 0.004.
The roundings to bfloat16 on the way count: a program that leaves them out, or rounds other values in their place, can miss the bound.
Values may be sent and summed in bfloat16 or wider, within the bound.
A program may use at most 128 MiB of HBM per device.

v0:
```python
import math

import jax
import jax.numpy as jnp
from jax import lax
from jax.sharding import Mesh
from jax.sharding import PartitionSpec as P

BLOCK = 64
BATCH = ("batch_0", "batch_1", "batch_2")


def shifted(block, axis, distance):
    devices = range(lax.axis_size(axis))
    route = [(i - distance, i) for i in devices if i - distance in devices]
    return lax.ppermute(block, axis, route)


def prefix(array, axis, combine, identity):
    peers, position = (lax.axis_size(axis), lax.axis_index(axis))
    everything = jax.tree.map(lambda part: lax.all_gather(part, axis), array)
    start = jax.tree.map(
        lambda part, zero: jnp.broadcast_to(jnp.asarray(zero, part.dtype), part.shape),
        array,
        identity,
    )

    def step(k, before):
        reached = k < position
        new = combine(before, jax.tree.map(lambda part: part[k], everything))
        return jax.tree.map(lambda a, b: jnp.where(reached, a, b), new, before)

    return lax.fori_loop(0, peers, step, start)


def gathered_by_axis(array, axes, dim):
    out = array
    for number in range(len(axes) - 1, -1, -1):
        out = lax.all_gather(out, axes[number], axis=dim, tiled=True)
    return out


def linear_blocks(lifted_query, key_heads, value_heads, log_decay, starts, initial):
    groups, length, head_count, key_width = lifted_query.shape
    value_width = value_heads.shape[3]
    block_count = length // BLOCK

    def split(member):
        return jnp.swapaxes(member.reshape((groups, block_count, BLOCK) + member.shape[2:]), 0, 1)

    def advance(carried, pieces):
        query_rows, key_rows, value_rows, log_rows, start_rows = pieces
        running = jnp.cumsum(log_rows, axis=1)
        segment_rank = jnp.cumsum(start_rows, axis=1)
        unbroken = (segment_rank == 0).astype(jnp.float32)
        raised_q = query_rows * jnp.exp(running)
        raised_k = key_rows * jnp.exp(-running)
        scores = jnp.einsum("gthc,gshc->ghts", raised_q, raised_k, precision=lax.Precision.HIGHEST)
        order = jnp.arange(BLOCK)
        causal = order[:, None] >= order[None, :]
        same_doc = segment_rank[:, :, None] == segment_rank[:, None, :]
        allowed = jnp.logical_and(causal[None], same_doc).astype(jnp.float32)
        inside = jnp.einsum(
            "ghts,gshv->gthv",
            scores * allowed[:, None],
            value_rows,
            precision=lax.Precision.HIGHEST,
        )
        outside = unbroken[:, :, None, None] * jnp.einsum(
            "gthc,ghcv->gthv", raised_q, carried, precision=lax.Precision.HIGHEST
        )
        final_log = running[:, -1]
        in_last = (segment_rank == segment_rank[:, -1:]).astype(jnp.float32)
        weighted = key_rows * jnp.exp(final_log[:, None] - running) * in_last[:, :, None, None]
        kept = unbroken[:, -1][:, None, None, None] * jnp.exp(final_log)[..., None] * carried
        updated = kept + jnp.einsum(
            "gshc,gshv->ghcv", weighted, value_rows, precision=lax.Precision.HIGHEST
        )
        return (updated, inside + outside)

    members = (lifted_query, key_heads, value_heads, log_decay, starts)
    final, outputs = lax.scan(advance, initial, tuple((split(member) for member in members)))
    outputs = jnp.swapaxes(outputs, 0, 1).reshape(groups, length, head_count, value_width)
    return (outputs, final)


def combine(earlier, later):
    return (earlier[0] * later[0], later[0][..., None] * earlier[1] + later[1])


def local(queries, keys, values, gate_rate, segment_ids, decay_exps, out_weight):
    groups = queries.shape[0]
    length = queries.shape[1]
    head_count = decay_exps.shape[0]

    def heads_of(array):
        return array.astype(jnp.float32).reshape(groups, length, head_count, -1)

    scaling = jnp.exp2(-decay_exps.astype(jnp.float32)) / 16.0
    log_decay = -heads_of(gate_rate) * scaling[None, None, :, None]
    prior = shifted(segment_ids[:, -1:] + 1, "seq", 1) - 1
    previous = jnp.concatenate([prior, segment_ids[:, :-1]], axis=1)
    starts = (segment_ids != previous).astype(jnp.float32)
    key_heads = heads_of(keys)
    value_heads = heads_of(values)
    key_width = key_heads.shape[3]
    query_heads = heads_of(queries) * (1.0 / math.sqrt(key_width))
    initial = jnp.zeros((groups, head_count, key_width, value_heads.shape[3]), jnp.float32)
    local_out, local_state = linear_blocks(
        query_heads, key_heads, value_heads, log_decay, starts, initial
    )
    through = jnp.cumsum(log_decay, axis=1)
    unbroken = (jnp.cumsum(starts, axis=1) == 0).astype(jnp.float32)
    passing = unbroken[:, -1][:, None, None] * jnp.exp(through[:, -1])
    identity = (jnp.ones_like(passing), jnp.zeros_like(local_state))
    incoming = prefix((passing, local_state), "seq", combine, identity)[1]
    correction = unbroken[:, :, None, None] * jnp.einsum(
        "gthc,ghcv->gthv", query_heads * jnp.exp(through), incoming, precision=lax.Precision.HIGHEST
    )
    mixed = local_out + correction
    normed = mixed / jnp.sqrt(jnp.mean(mixed * mixed, axis=-1, keepdims=True) + 1.0)
    hidden = normed.astype(jnp.bfloat16).reshape(groups * length, -1)
    product = jnp.dot(
        hidden, gathered_by_axis(out_weight, BATCH, 0), preferred_element_type=jnp.float32
    )
    return product.astype(jnp.bfloat16).reshape(groups, length, -1)


def solution(mesh):
    split = Mesh(
        mesh.devices.reshape(mesh.shape["seq"], 8, 4, 4), ("seq", "batch_0", "batch_1", "batch_2")
    )
    return jax.shard_map(
        local,
        mesh=split,
        in_specs=(
            P(BATCH, "seq", None),
            P(BATCH, "seq", None),
            P(BATCH, "seq", None),
            P(BATCH, "seq", None),
            P(BATCH, "seq"),
            P(),
            P(BATCH, None),
        ),
        out_specs=P(BATCH, "seq", None),
        check_vma=False,
    )
```

profile of v0, /device:TPU:1, one launch (start us, length us, event | category | flops | bytes accessed | tf_op | source)
XLA Modules:
  0.0 288.8 jit_solution(386403750227344265)
XLA Ops:
  9.7 13.1 %all_gather.22 = bf16[64,2048]{1,0:T(8,128)(2,1)} all-gather(bf16[16,2048]{1,0:T(8,128)(2,1)} %param.17), channel_id=1, replica_groups=mesh['seq'=2,'batch_0'=8,'batch_1'=4,'batch_2'=4] {'batch_2'}, dimensions={0}, use_global_device_ids=true | all-gather | bytes 327680 | tf_op jit(solution)/shard_map/all_gather | solution.py:39
  22.9 1.5 copy.83
  24.4 1.6 convert_negate_fusion
  26.0 1.5 copy.85
  27.5 1.6 convert_multiply_fusion
  29.2 2.9 copy.84
  32.0 3.2 %neg.34 = f32[8,1,64,4,256]{4,3,2,0,1:T(4,128)} reshape(f32[1,512,1024]{2,1,0:T(8,128)} %copy.84) | data formatting | bytes 4194304 | tf_op jit(solution)/shard_map/neg | solution.py:100
  35.2 4.4 %reshape.392 = f32[8,1,64,4,256]{2,0,4,3,1:T(8,128)} reshape(f32[1,512,1024]{1,2,0:T(8,128)} %convert_multiply_fusion) | data formatting | bytes 4194304 | tf_op jit(solution)/shard_map/mul | solution.py:107
  39.6 4.0 %copy.89 = f32[8,1,64,4,256]{4,3,2,1,0:T(4,128)} copy(f32[8,1,64,4,256]{2,0,4,3,1:T(8,128)} %reshape.392) | data formatting | bytes 4194304
  43.6 6.1 %reshape.386 = f32[8,1,64,4,512]{4,3,2,0,1:T(4,128)} reshape(bf16[1,512,2048]{2,1,0:T(8,128)(2,1)} %param.13) | data formatting | bytes 6291456 | tf_op jit(solution)/shard_map/transpose;reshape;reshape | solution.py:49
  49.7 1.9 reshape.385
  51.6 3.4 %multiply_bitcast_fusion.2 = f32[8,1,64,4,256]{4,3,2,1,0:T(4,128)} fusion(f32[8,1,64,4,256]{4,3,2,0,1:T(4,128)} %neg.34, f32[4]{0:T(128)S(1)} %exponential_multiply_fusion.1), kind=kLoop, calls=%fused_computation.60 | loop fusion | flops 524288 | bytes 4194320
  56.8 93.7 %while.27 = (s32[]{:T(128)}, f32[1,4,256,512]{3,2,1,0:T(8,128)S(1)}, f32[8,1,64,4,512]{4,2,0,3,1:T(8,128)}, f32[8,1,64]{2,1,0:T(1,128)S(1)}, f32[8,1,64,4,256]{4...) while((s32[]{:T(128)}, ...), condition=%wide.region_3.4_spmd.clone, body=%wide.region_0.3_spmd.clone.sunk | while | flops 963220736 | bytes 13299679 | solution.py:82
  63.5 1.6 fusion.70
  66.2 2.3 bitcast_add_fusion.7
  72.7 1.4 fusion.68
  75.3 1.6 fusion.70
  78.0 2.3 bitcast_add_fusion.7
  84.5 1.4 fusion.68
  87.0 1.6 fusion.70
  89.7 2.3 bitcast_add_fusion.7
  98.7 1.6 fusion.70
  101.4 2.3 bitcast_add_fusion.7
  107.9 1.4 fusion.68
  110.4 1.6 fusion.70
  113.1 2.3 bitcast_add_fusion.7
  119.6 1.4 fusion.68
  122.1 1.6 fusion.70
  124.8 2.3 bitcast_add_fusion.7
  131.3 1.4 fusion.68
  133.8 1.6 fusion.70
  136.5 2.3 bitcast_add_fusion.7
  145.5 1.6 fusion.70
  148.2 2.3 bitcast_add_fusion.7
  152.6 3.3 %multiply_bitcast_fusion.1 = f32[1,256,4,512]{3,1,2,0:T(8,128)} fusion(f32[1,512,4,256]{1,3,2,0:T(8,128)} %bitcast.179, f32[4]{0:T(128)S(1)} %exponential_multiply_fusion.1), kind=kLoop, calls=%fused_computation.58 | loop fusion | flops 524288 | bytes 4194320 | tf_op jit(solution)/shard_map/transpose
  155.9 2.9 %copy.91 = f32[1,256,4,512]{1,3,2,0:T(8,128)} copy(f32[1,256,4,512]{3,1,2,0:T(8,128)} %multiply_bitcast_fusion.1) | data formatting | bytes 4194304 | tf_op jit(solution)/shard_map/transpose
  158.8 2.9 %fusion.35 = f32[1,256,4,4,128]{1,3,2,4,0:T(4,128)S(1)} fusion(f32[1,256,4,4,128]{1,4,3,2,0:T(8,128)} %bitcast.180), kind=kOutput, calls=%fused_computation.55 | output fusion | flops 66584576 | bytes 4194304 | tf_op jit(solution)/shard_map/reduce-window.2
  161.8 2.5 copy.93
  164.3 2.9 copy.97
  167.2 6.7 %multiply_bitcast_fusion = (f32[512,4,256]{2,1,0:T(4,128)}, f32[1,256,4,512]{1,2,3,0:T(4,128)}) fusion(f32[1,512,4,256]{3,2,1,0:T(4,128)} %copy.97, f32[256,4,4]{0,1,2:T(4,128)S(1)} %copy.94, f32[1,256,4,512]{1,3,2,0:T(8,128)} %bitcast.181), kind=kLoop, calls=%fused_computation.57 | loop fusion | flops 1048576 | bytes 8404992 | tf_op jit(solution)/shard_map/reshape.37
  177.2 5.2 %copy.100 = f32[1,512,4,512]{1,3,2,0:T(8,128)} copy(f32[1,512,4,512]{3,1,2,0:T(8,128)} %bitcast.182) | data formatting | bytes 8388608 | tf_op jit(solution)/shard_map/reshape;transpose | solution.py:83
  183.2 6.3 %all_gather.19 = f32[2,1,4,256]{3,2,1,0:T(4,128)S(1)} all-gather(f32[1,1,4,256]{3,2,1,0:T(4,128)S(1)} %fusion.37), channel_id=1, replica_groups=mesh['seq'=2,'batch_0'=8,'batch_1'=4,'batch_2'=4] {'seq'}, dimensions={0}, use_global_device_ids=true | all-gather | bytes 12288 | tf_op jit(solution)/shard_map/all_gather | solution.py:21
  189.5 4.5 %while.28 = (s32[]{:T(128)}, f32[1,4,256,512]{3,2,1,0:T(8,128)S(1)}, s32[]{:T(128)}, f32[2,1,4,256]{3,2,1,0:T(4,128)S(1)}, f32[2,1,4,256,512]{4,3,2,1,0:T(8,128)}, /*index=5*/s32[]{:T(128)}, s32[]{:T(128)}) while((s32[]{:T(128)}, f32[1,4,256,512]{3,2,1,0:T(8,128)S(1)}, s32[]{:T(128)}, f32[2,1,4,256]{3,2,1,0:T(4,128)S(1)}, ...), condition=%wide.region_9.10_spmd.clone, body=%wide.region_8.9_spmd.clone.sunk | while | flops 2097156 | bytes 6303849 | solution.py:33
  189.5 2.2 fusion.71
  191.8 2.2 fusion.71
  194.0 9.6 %multiply_reduce_fusion = (f32[512,4]{0,1:T(4,128)S(1)}, f32[1,512,4,512]{1,3,2,0:T(8,128)S(1)}) fusion(f32[1,512,4,512]{1,3,2,0:T(8,128)} %copy.100, f32[512,4,256]{2,1,0:T(4,128)} %get-tuple-element.281, f32[1,4,256,512]{3,2,1,0:T(8,128)S(1)} %get-tuple-element.144, f32[512]{0:T(512)S(1)} %fusion.39), kind=kOutput, calls=%fused_computation.49 | convolution fusion | flops 3225417728 | bytes 12593152 | tf_op jit(solution)/shard_map/gthc,ghcv->gthv/dot_general | solution.py:117
  204.2 68.9 %all-gather.7.cloned.1.call-done = bf16[2048,2048]{1,0:T(8,128)(2,1)} async-done(((bf16[256,2048]{1,0:T(8,128)(2,1)}), bf16[2048,2048]{1,0:T(8,128)(2,1)}) %all-gather.7.cloned.1.call-update) | async-done | bytes 8388624 | tf_op jit(solution)/shard_map/all_gather | solution.py:39
  273.1 9.1 %fusion.32 = bf16[1,512,2048]{2,1,0:T(8,128)(2,1)} fusion(bf16[512,2048]{0,1:T(8,128)(2,1)S(1)} %bitcast.184, bf16[2048,2048]{1,0:T(8,128)(2,1)} %all-gather.7.cloned.1.call-done), kind=kOutput, calls=%fused_computation.51 | convolution fusion | flops 4296015872 | bytes 12582912 | tf_op jit(solution)/shard_map/dot_general | solution.py:123
  (150 shorter events, 60.0 us)
Async XLA Ops:
  6.5 145.6 %all-gather.5.cloned.1.call-start = ((), (), s32[]{:S(2)}) async-start(), calls=%async_computation | async-start | bytes 1310720 | tf_op jit(solution)/shard_map/all_gather | solution.py:39
  8.4 46.6 %collective-permute-start = (s32[1,1]{1,0:T(1,128)}, s32[1,1]{1,0:T(1,128)}, u32[]{:S(2)}, u32[]{:S(2)}) collective-permute-start(s32[1,1]{1,0:T(1,128)} %add.59), channel_id=1, source_target_pairs={{0,128},{1,129},{2,130},{3,131},{4,132},{5,133},{6,134},{7,135},{8... | collective-permute-start | bytes 20 | tf_op jit(solution)/shard_map/ppermute | solution.py:16
  22.8 166.7 %all-gather.9.cloned.1.call-start = ((), (), s32[]{:S(2)}) async-start(), calls=%async_computation.2 | async-start | bytes 6291456 | tf_op jit(solution)/shard_map/all_gather | solution.py:21
  24.4 1.6 copy-start.3
  43.6 6.1 %copy-start.1 = (bf16[1,512,1024]{2,1,0:T(8,128)(2,1)S(1)}, bf16[1,512,1024]{2,1,0:T(8,128)(2,1)}, u32[]{:S(2)}) copy-start(bf16[1,512,1024]{2,1,0:T(8,128)(2,1)} %param.12) | copy-start | bytes 3145732
  51.6 4.5 %copy-start.2 = (s32[1,512]{1,0:T(1,128)S(1)}, s32[1,512]{1,0:T(1,128)}, u32[]{:S(2)}) copy-start(s32[1,512]{1,0:T(1,128)} %param.15) | copy-start | bytes 6148
  150.5 1.3 copy-start
  151.9 121.2 %all-gather.7.cloned.1.call-start = ((), (), s32[]{:S(2)}) async-start(), calls=%async_computation.1 | async-start | bytes 9437184 | tf_op jit(solution)/shard_map/all_gather | solution.py:39
Sparse Core Ops, SparseCore 0:
  22.9 29.7 all-gather.4
  152.0 24.7 all-gather.8
  178.6 94.4 all-gather.6
where the time goes:
time: 291 us; the launch traced here: 289 us
  waiting for transfers between devices  69.5 us (24%)
  matrix products  64.5 us (22%)
  local copies, waits for them, and re-layouts  61.3 us (21%)
  other arithmetic  51.9 us (18%)
  blocking collectives  19.3 us (7%)
  between operations  15.7 us (5%)
  loops' own time  5.01 us (2%)
    all_gather x2, waiting for transfers between devices, gathered_by_axis(): out = lax.all_gather(out, axes[number], axis=dim, tiled=True)  69 us
    dot_general x8, matrix products, advance(): jnp.einsum('gshc,gshv->ghcv', weighted, value_rows, precision=lax.Precisi...  18.2 us
    all_gather x1, blocking collectives, gathered_by_axis(): out = lax.all_gather(out, axes[number], axis=dim, tiled=True)  13.1 us
    dot_general x8, matrix products, advance(): jnp.einsum('ghts,gshv->gthv', scores * allowed[:, None], value_rows, prec...  12.6 us
    dot_general x8, matrix products, advance(): jnp.einsum('gthc,ghcv->gthv', raised_q, carried, precision=lax.Precision....  11.5 us
    another operation x5, other arithmetic  10.2 us
    mul x8, other arithmetic, advance(): raised_k = key_rows * jnp.exp(-running)  10.1 us
    dot_general x1, matrix products, local(): jnp.einsum('gthc,ghcv->gthv', query_heads * jnp.exp(through), incoming, p...  9.59 us
  transfers between devices with their start and end apart: 4, of which 1 were waited for; matrix products, arithmetic and copies ran while one was open for 57% of the time, Pallas kernels for 0%

commit v1 on v0

v1 whole, which is shorter than its diff:
```python
import functools
import math

import jax
import jax.numpy as jnp
from jax import lax
from jax.experimental import pallas as pl
from jax.experimental.pallas import tpu as pltpu
from jax.sharding import Mesh
from jax.sharding import PartitionSpec as P

BLOCK = 256
F32, BF16 = jnp.float32, jnp.bfloat16


def halves(x):
    high = x.astype(BF16)
    return high, (x - high.astype(F32)).astype(BF16)


def dot(a, b, dims):
    return lax.dot_general(a, b, (dims, ((), ())), preferred_element_type=F32)


def decay_rate(decay_ref, h, width):
    exponent = jnp.full((1, width), decay_ref[h], jnp.int32).astype(F32)
    return -(jnp.exp2(-exponent) / 16.0)


def running_log(gate, rate):
    rows = lax.broadcasted_iota(jnp.int32, (BLOCK, BLOCK), 0)
    cols = lax.broadcasted_iota(jnp.int32, (BLOCK, BLOCK), 1)
    triangle = jnp.where(rows >= cols, 1.0, 0.0).astype(BF16)
    parts, carry = [], None
    for b in range(gate.shape[0] // BLOCK):
        part = dot(triangle, gate[b * BLOCK : (b + 1) * BLOCK], ((1,), (0,)))
        if carry is not None:
            part = part + carry
        carry = part[BLOCK - 1 :]
        parts.append(part)
    return jnp.concatenate(parts, axis=0) * rate


def column(row, width):
    return jnp.transpose(jnp.broadcast_to(row, (width, row.shape[1])))


def state_of(k, v, log, same):
    weight = k.astype(F32) * jnp.exp(log[-1:] - log) * same
    high, low = halves(weight)
    return dot(jnp.concatenate([high, low], axis=0), jnp.concatenate([v, v], axis=0), ((0,), (0,)))


def inside(q_high, q_low, k_high, k_low, v, seg_row, seg_col, b):
    here, upto = b * BLOCK, (b + 1) * BLOCK
    qh, ql = q_high[here:upto], q_low[here:upto]
    kh, kl = k_high[:upto], k_low[:upto]
    scores = dot(
        jnp.concatenate([qh, qh, ql], axis=1), jnp.concatenate([kh, kl, kh], axis=1), ((1,), (1,))
    )
    rows = lax.broadcasted_iota(jnp.int32, scores.shape, 0) + here
    cols = lax.broadcasted_iota(jnp.int32, scores.shape, 1)
    seg_t = jnp.concatenate([seg_col[here:upto]] * (upto // 128), axis=1)
    allowed = jnp.logical_and(rows >= cols, seg_t == seg_row[:, :upto])
    high, low = halves(jnp.where(allowed, scores, 0.0))
    return dot(
        jnp.concatenate([high, low], axis=1), jnp.concatenate([v[:upto], v[:upto]], axis=0), ((1,), (0,))
    )


def state_kernel(key_width, value_width, heads, decay_ref, seg_ref, k_ref, g_ref, v_ref, s_ref):
    @pl.when(lax.axis_index("seq") == 0)
    def _():
        seg_col = column(seg_ref[...].astype(F32), 128)
        same = (seg_col == seg_col[-1:]).astype(F32)
        same = jnp.concatenate([same] * (key_width // 128), axis=1)
        for h in range(heads):
            ks, vs = pl.ds(h * key_width, key_width), pl.ds(h * value_width, value_width)
            log = running_log(g_ref[:, ks], decay_rate(decay_ref, h, key_width))
            s_ref[h] = state_of(k_ref[:, ks], v_ref[:, vs], log, same)


def mix_kernel(key_width, value_width, heads, decay_ref, prior_ref, seg_ref, q_ref, k_ref, g_ref, v_ref, s_ref, o_ref):
    seg_row = seg_ref[...].astype(F32)
    seg_col = column(seg_row, 128)
    going = (seg_col == prior_ref[...].astype(F32)).astype(F32)
    going = jnp.concatenate([going] * (value_width // 128), axis=1)
    for h in range(heads):
        ks, vs = pl.ds(h * key_width, key_width), pl.ds(h * value_width, value_width)
        log = running_log(g_ref[:, ks], decay_rate(decay_ref, h, key_width))
        q_high, q_low = halves(q_ref[:, ks].astype(F32) * (1.0 / math.sqrt(key_width)) * jnp.exp(log))
        k_high, k_low = halves(k_ref[:, ks].astype(F32) * jnp.exp(-log))
        v = v_ref[:, vs]
        mixed = jnp.concatenate(
            [
                inside(q_high, q_low, k_high, k_low, v, seg_row, seg_col, b)
                for b in range(q_high.shape[0] // BLOCK)
            ],
            axis=0,
        )
        s_high, s_low = halves(s_ref[h])
        mixed = mixed + going * dot(
            jnp.concatenate([q_high, q_high, q_low], axis=1),
            jnp.concatenate([s_high, s_low, s_high], axis=0),
            ((1,), (0,)),
        )
        square = jnp.sum(mixed * mixed, axis=1, keepdims=True) * (1.0 / value_width)
        o_ref[:, vs] = (mixed / jnp.sqrt(square + 1.0)).astype(BF16)


def local(queries, keys, values, gate_rate, segment_ids, decay_exps, out_weight):
    length, heads = queries.shape[1], decay_exps.shape[0]
    key_width, value_width = queries.shape[2] // heads, values.shape[2] // heads
    q, k, g, v = queries[0], keys[0], gate_rate[0], values[0]
    whole = pl.BlockSpec(memory_space=pltpu.VMEM)
    scalar = pl.BlockSpec(memory_space=pltpu.SMEM)
    params = pltpu.CompilerParams(vmem_limit_bytes=60 * 1024 * 1024)
    weight = lax.all_gather(out_weight, ("batch_0", "batch_1", "batch_2"), axis=0, tiled=True)
    state = pl.pallas_call(
        functools.partial(state_kernel, key_width, value_width, heads),
        out_shape=jax.ShapeDtypeStruct((heads, key_width, value_width), F32),
        in_specs=[scalar] + [whole] * 4,
        out_specs=whole,
        compiler_params=params,
        name="state",
    )(decay_exps, segment_ids, k, g, v)
    incoming = lax.ppermute(state, "seq", [(0, 1)])
    prior = lax.ppermute(segment_ids[:, -1:] + 1, "seq", [(0, 1)]) - 1
    hidden = pl.pallas_call(
        functools.partial(mix_kernel, key_width, value_width, heads),
        out_shape=jax.ShapeDtypeStruct((length, heads * value_width), BF16),
        in_specs=[scalar] + [whole] * 7,
        out_specs=whole,
        compiler_params=params,
        name="mix",
    )(decay_exps, prior, segment_ids, q, k, g, v, incoming)
    product = jnp.dot(hidden, weight, preferred_element_type=F32)
    return product.astype(BF16)[None]


def solution(mesh):
    split = Mesh(
        mesh.devices.reshape(mesh.shape["seq"], 8, 4, 4), ("seq", "batch_0", "batch_1", "batch_2")
    )
    batch = ("batch_0", "batch_1", "batch_2")
    return jax.shard_map(
        local,
        mesh=split,
        in_specs=(P(batch, "seq", None),) * 4 + (P(batch, "seq"), P(), P(batch, None)),
        out_specs=P(batch, "seq", None),
        check_vma=False,
    )
```

time: 291 us -> 155 us (0.53)
  local copies, waits for them, and re-layouts: 61.3 us -> 2.57 us
  matrix products: 64.5 us -> 9.83 us
  other arithmetic: 51.9 us -> 0 us
  waiting for transfers between devices: 69.5 us -> 107 us
  blocking collectives: 19.3 us -> 0 us
  Pallas kernels: 0 us -> 15.6 us
  loops' own time: 5.01 us -> 0 us
    dot_general x34 -> x1, matrix products: 64.5 us -> 9.83 us  [local(): product = jnp.dot(hidden, weight, preferred_element_type=F32)]
    all_gather x3 -> x1, waiting for transfers between devices: 69 us -> 99.3 us  [local(): lax.all_gather(out_weight, ('batch_0', 'batch_1', 'batch_2'), axis=0, til...]
    another operation x21 -> x0, other arithmetic: 20.4 us -> none
    all_gather x2 -> x0, blocking collectives: 19.3 us -> none  [the longest x1 13.1 us: gathered_by_axis(): out = lax.all_gather(out, axes[number], axis=dim, tiled=True)]
    another operation x10 -> x0, local copies, waits for them, and re-layouts: 16 us -> none  [the longest x3 8.1 us: split(): jnp.swapaxes(member.reshape((groups, block_count, BLOCK) + member.shape[2...]
    pallas_call x0 -> x2, Pallas kernels: none -> 15.6 us  [the longest x1 12 us: local(): pl.pallas_call(functools.partial(mix_kernel, key_width, value_width, head...]
    mul x18 -> x0, other arithmetic: 12.4 us -> none  [the longest x8 10.1 us: advance(): raised_k = key_rows * jnp.exp(-running)]
    slice x20 -> x1, local copies, waits for them, and re-layouts: 11.6 us -> 1.26 us  [local(): prior = lax.ppermute(segment_ids[:, -1:] + 1, 'seq', [(0, 1)]) - 1]
  transfers between devices with their start and end apart: 4 -> 3, of which waited for: 1 -> 2; matrix products, arithmetic and copies ran while one was open for 57% -> 1% of each run, Pallas kernels for 0% -> 10%
where the time goes in v1:
time: 155 us; the launch traced here: 152 us
  waiting for transfers between devices  107 us (69%)
  Pallas kernels  15.6 us (10%)
  between operations  14.7 us (9%)
  matrix products  9.83 us (6%)
  starting transfers between devices  2.76 us (2%)
  local copies, waits for them, and re-layouts  2.57 us (2%)
    all_gather x1, waiting for transfers between devices, local(): lax.all_gather(out_weight, ('batch_0', 'batch_1', 'batch_2'), axis=0, til...  99.3 us
    pallas_call x1, Pallas kernels, local(): pl.pallas_call(functools.partial(mix_kernel, key_width, value_width, head...  12 us
    dot_general x1, matrix products, local(): product = jnp.dot(hidden, weight, preferred_element_type=F32)  9.83 us
    ppermute x1, waiting for transfers between devices, local(): prior = lax.ppermute(segment_ids[:, -1:] + 1, 'seq', [(0, 1)]) - 1  6.57 us
    pallas_call x1, Pallas kernels, local(): pl.pallas_call(functools.partial(state_kernel, key_width, value_width, he...  3.6 us
  transfers between devices with their start and end apart: 3, of which 2 were waited for; matrix products, arithmetic and copies ran while one was open for 1% of the time, Pallas kernels for 10%

profile of v1, /device:TPU:1, one launch (start us, length us, event | category | flops | bytes accessed | tf_op | source)
XLA Modules:
  0.0 152.0 jit_solution(7061698702032235903)
XLA Ops:
  6.5 0.0 all-gather.2.cloned.1.call-start
  6.5 0.7 all-gather.2.cloned.1.call-update
  7.3 3.6 %state.1 = f32[4,256,512]{2,1,0:T(8,128)} custom-call(s32[4]{0:T(128)} %decay_ref.3, s32[1,512]{1,0:T(1,128)} %seg_ref.3, bf16[512,1024]{1,0:T(8,128)(2,1)} %bitcast.10, bf16[512,1024]{1,0:T(8,128)(2,1)} %bitcast.12, bf16[512,2048]{1,0:T(8,128)(2,1)} %bitcast.8), custom_call_target="tpu_custom_call" | custom-call | tf_op jit(solution)/shard_map/state/pallas_call | solution.py:119
  10.9 1.3 collective-permute-start.1
  12.1 1.3 slice.3
  14.0 1.5 collective-permute-start
  15.5 6.6 %collective-permute-done = s32[1,1]{1,0:T(1,128)} collective-permute-done((s32[1,1]{1,0:T(1,128)}, s32[1,1]{1,0:T(1,128)}, u32[]{:S(2)}, u32[]{:S(2)}) %collective-permute-start) | collective-permute-done | bytes 36 | tf_op jit(solution)/shard_map/ppermute | solution.py:128
  22.7 0.0 collective-permute-done.1.s_ref
  22.7 0.0 copy-start
  22.7 1.3 copy-done
  24.1 12.0 %mix.1 = bf16[512,2048]{1,0:T(8,128)(2,1)} custom-call(s32[4]{0:T(128)} %decay_ref.3, s32[1,1]{1,0:T(1,128)S(6)} %sub.3.prior_ref, s32[1,512]{1,0:T(1,128)} %seg_ref.3, bf16[512,1024]{1,0:T(8,128)(2,1)} %bitcast.14, bf16[512,1024]{1,0:T(8,128)(2,1)} %bitcast.11, bf16[512,1024]{1,0:T(8,128)(2,1)} %bitcast.13, bf16[512,2048]{1,0:T(8,128)(2,1)} %bitcast.9, ...), custom_call_target="tpu_custom_call" | custom-call | tf_op jit(solution)/shard_map/mix/pallas_call | solution.py:129
  36.0 99.3 %all-gather.2.cloned.1.call-done = bf16[2048,2048]{1,0:T(8,128)(2,1)} async-done(((bf16[16,2048]{1,0:T(8,128)(2,1)}), bf16[2048,2048]{1,0:T(8,128)(2,1)}) %all-gather.2.cloned.1.call-update) | async-done | bytes 8388624 | tf_op jit(solution)/shard_map/all_gather | solution.py:118
  135.3 9.8 %fusion = bf16[1,512,2048]{2,1,0:T(8,128)(2,1)} fusion(bf16[512,2048]{1,0:T(8,128)(2,1)} %mix.1, bf16[2048,2048]{1,0:T(8,128)(2,1)} %all-gather.2.cloned.1.call-done), kind=kOutput, calls=%fused_computation.1 | convolution fusion | flops 4296015872 | bytes 12582912 | tf_op jit(solution)/shard_map/dot_general | solution.py:137
Async XLA Ops:
  6.5 128.8 %all-gather.2.cloned.1.call-start = ((), (), s32[]{:S(2)}) async-start(), calls=%async_computation | async-start | bytes 8454144 | tf_op jit(solution)/shard_map/all_gather | solution.py:118
  10.9 11.9 %collective-permute-start.1 = (f32[4,256,512]{2,1,0:T(8,128)}, f32[4,256,512]{2,1,0:T(8,128)S(1)}, u32[]{:S(2)}, u32[]{:S(2)}) collective-permute-start(f32[4,256,512]{2,1,0:T(8,128)} %state.1), channel_id=1, source_target_pairs={{0,128},{1,129},{2,130},{3,131},{4,132},{5,133},{6,134},{7,135},{8... | collective-permute-start | bytes 6291464 | tf_op jit(solution)/shard_map/ppermute | solution.py:127
  14.0 8.0 %collective-permute-start = (s32[1,1]{1,0:T(1,128)}, s32[1,1]{1,0:T(1,128)}, u32[]{:S(2)}, u32[]{:S(2)}) collective-permute-start(s32[1,1]{1,0:T(1,128)} %add.4), channel_id=1, source_target_pairs={{0,128},{1,129},{2,130},{3,131},{4,132},{5,133},{6,134},{7,135},{8... | collective-permute-start | bytes 20 | tf_op jit(solution)/shard_map/ppermute | solution.py:128
  22.7 1.3 copy-start
Sparse Core Ops, SparseCore 0:
  11.0 124.3 all-gather.1
